TPU v7x, 256 devices: a 2x2x32 block of a 4x8x32 slice. The times are simulated.
256 devices in a mesh: member: 4 (over y, x), node: 64 (over z, core).
Axes of the slice: x: 2, y: 2, z: 32, core: 2. Of those that a mesh axis runs over, the one named last changes fastest.
The devices are a block of a 4x8x32 slice.
Arguments:
- conditioning: bfloat16 [168, 262144], P(None, ('member', 'node')), parts along dimension 1, may hold values from -6 to 6
- target_state: float32 [84, 262144], P(None, ('member', 'node')), parts along dimension 1, may hold values from -6 to 6
- noise_sample: float32 [84, 262144], P(None, ('member', 'node')), parts along dimension 1, may hold values from -6 to 6
- step_index: int32 [4], P('member'), parts along dimension 0, may hold values from 0 to 19
- mesh_features: float32 [3, 40960], P(None, 'node'), may hold values from -1 to 1
- edge_geometry: float32 [4, 262144], P(None, 'node'), may hold values from -6 to 6
- edge_slot: int32 [262144], P('node'), may hold values from 0 to 1023, as said below
- edge_receiver: int32 [262144], P('node'), may hold values from 0 to 639
- send_rows: int32 [4096, 16], P('node'), may hold values from 0 to 1023
- edge_count: int32 [64], P('node'), may hold values from 1503 to 4096, as said below
- embed_weight: bfloat16 [252, 512], replicated, may hold values from -0.375 to 0.375
- mesh_weight: float32 [3, 512], replicated, may hold values from -3.5 to 3.5
- geom_weight: float32 [4, 512], replicated, may hold values from -3 to 3
- sender_weight: bfloat16 [512, 512], P('node'), may hold values from -0.15625 to 0.15625
- edge_weight: bfloat16 [512, 512], P('node'), may hold values from -0.15625 to 0.15625
- receiver_weight: bfloat16 [512, 512], P('node'), may hold values from -0.15625 to 0.15625
- message_weight: bfloat16 [512, 512], P('node'), may hold values from -0.25 to 0.25
- node_weight: bfloat16 [1024, 512], P('node'), may hold values from -0.1875 to 0.1875
- output_weight: bfloat16 [512, 512], P('node'), may hold values from -0.25 to 0.25
- noise_weight: float32 [32, 512], replicated, may hold values from -1 to 1
- film_weight: bfloat16 [512, 2048], replicated, may hold values from -0.25 to 0.25
Outputs:
- mesh_latent: bfloat16 [40960, 2048], P('node', 'member'), parts along dimension 1
There are 4 independent parts, one for each index of `member`. A program takes and returns all parts, laid end to end along the dimension named above; an argument that names none is the same for every part. Nothing has to cross between parts.
Inputs may be any that keep to these rules, and one draw needn't show every extreme that they name: `edge_slot`: on each device, the live slots name every entry of its 64 * 16 list at least once, or as many distinct entries as there are live slots where these are fewer. `edge_count`: the counts sum to 64 * 2048 and one device has all 4096 slots live.
All inputs are finite; a program needn't handle non-finite values.
Results may differ from a plain program's by a relative error of at most 0.0071.
Values may be sent and summed in bfloat16 or wider, within the bound.
A program may use at most 64 MiB of HBM per device.

v0:
```python
import functools

import jax
import jax.numpy as jnp
from jax import lax
from jax.experimental import pallas as pl
from jax.experimental.pallas import tpu as pltpu
from jax.sharding import PartitionSpec as P

STEPS = 20
sigma_top = 80.0
sigma_low = 0.03
rho_power = 7.0
norm_eps = 1e-05
MESH = pl.DeviceIdType.MESH
VMEM = pl.BlockSpec(memory_space=pltpu.VMEM)
SMEM = pl.BlockSpec(memory_space=pltpu.SMEM)
ANY = pl.BlockSpec(memory_space=pl.ANY)
LIMIT = 60 * 1024 * 1024
f32, bf16 = jnp.float32, jnp.bfloat16


def silu(x):
    half = 0.5 * x
    return half + half * jnp.tanh(half)


def turned(x):
    return x.astype(f32).T


def pick_kernel(scal, cond, target, noise, rows, out, raw):
    chans, points = raw.shape
    vars_ = target.shape[0]
    lead = chans - cond.shape[0]
    noisy = (target[...] + scal[0] * noise[...]) / scal[1]
    raw[0:vars_] = noisy
    if lead > vars_:
        raw[vars_:lead] = jnp.zeros((lead - vars_, points), f32)
    raw[lead:chans] = cond[...].astype(f32)
    picks = rows.shape[1]
    values = raw[...].astype(bf16)
    ids = lax.broadcasted_iota(jnp.int32, (points, picks), 0)
    one_hot = jnp.where(ids == rows[...], 1.0, 0.0).astype(bf16)
    out[...] = jnp.dot(values, one_hot, preferred_element_type=f32).T.astype(bf16)


def exchange_kernel(
    devices, x, wa, wb, wc, wd, wo, wn, o, w_all, w_node,
    local, ready_r, ready_l, pair, send, recv, ring_s, ring_r, part_s, part_r,
):
    chips = devices // 2
    half = chips // 2
    me = lax.axis_index("node")
    z, c = me // 2, lax.rem(me, 2)
    right, left = lax.rem(me + 2, devices), lax.rem(me + devices - 2, devices)
    part = z * 2 + 1 - c
    barrier = pltpu.get_barrier_semaphore()
    for t in (right, left, part):
        pl.semaphore_signal(barrier, inc=1, device_id={"node": t}, device_id_type=MESH)
    rows = wa.shape[0]
    width = wa.shape[1]
    node_rows = wn.shape[0]
    cap = x.shape[0] // devices

    def place(n):
        return w_all.at[pl.ds(pl.multiple_of(n * rows, rows), rows)]

    def place_node(n):
        return w_node.at[pl.ds(pl.multiple_of(n * node_rows, node_rows), node_rows)]

    own = [
        pltpu.make_async_copy(w, place(me).at[:, width * k : width * (k + 1)], local.at[k])
        for k, w in enumerate((wa, wb, wc, wd, wo))
    ]
    own.append(pltpu.make_async_copy(wn, place_node(me), local.at[5]))

    def block(ref, n):
        return ref.at[pl.ds(pl.multiple_of(n * cap, cap), cap)]

    own.append(pltpu.make_async_copy(block(x, me), block(o, me), local.at[6]))
    for copy in own:
        copy.start()
    for copy in own:
        copy.wait()
    pl.semaphore_wait(barrier, 3)
    pl.semaphore_signal(pair, inc=1, device_id={"node": part}, device_id_type=MESH)

    def ring(direction, n, s, target):
        return [
            pltpu.make_async_remote_copy(
                src_ref=ref(n), dst_ref=ref(n),
                send_sem=ring_s.at[direction, k, s], recv_sem=ring_r.at[direction, k, s],
                device_id={"node": target}, device_id_type=MESH,
            )
            for k, ref in enumerate((place, place_node))
        ]

    def to_part(i, n):
        return [
            pltpu.make_async_remote_copy(
                src_ref=ref(n), dst_ref=ref(n),
                send_sem=part_s.at[k, i], recv_sem=part_r.at[k, i],
                device_id={"node": part}, device_id_type=MESH,
            )
            for k, ref in enumerate((place, place_node))
        ]

    def points(i, target):
        return pltpu.make_async_remote_copy(
            src_ref=block(x, target), dst_ref=block(o, me),
            send_sem=send.at[i], recv_sem=recv.at[i],
            device_id={"node": target}, device_id_type=MESH,
        )

    def start(copies):
        for copy in copies:
            copy.start()

    start(ring(0, me, 0, right))
    start(ring(1, me, 0, left))
    pl.semaphore_wait(pair, 1)
    points(0, part).start()
    start(to_part(0, me))

    def chip(k):
        return lax.rem(z + k + 2 * chips, chips)

    def announce(k):
        @pl.when(k < half)
        def _():
            pl.semaphore_signal(ready_r.at[k + 1], inc=1, device_id={"node": left}, device_id_type=MESH)

        @pl.when(k < half - 1)
        def _():
            pl.semaphore_signal(ready_l.at[k + 1], inc=1, device_id={"node": right}, device_id_type=MESH)

    def offer(k):
        @pl.when(k > 1)
        def _():
            pl.semaphore_wait(ready_r.at[k], 1)

            @pl.when(k < half)
            def _():
                pl.semaphore_wait(ready_l.at[k], 1)

        announce(k)
        for other in (0, 1):
            points(k * 4 + other, chip(k) * 2 + lax.rem(c + other, 2)).start()

            @pl.when(k < half)
            def _():
                points(k * 4 + 2 + other, chip(-k) * 2 + lax.rem(c + other, 2)).start()

    def step(k, carry):
        n = chip(-k) * 2 + c
        for copy in ring(0, n, k - 1, right):
            copy.wait_recv()

        @pl.when(k < half)
        def _():
            start(ring(0, n, k, right))

        start(to_part(k, n))

        @pl.when(k < half)
        def _():
            m = chip(k) * 2 + c
            for copy in ring(1, m, k - 1, left):
                copy.wait_recv()

            @pl.when(k < half - 1)
            def _():
                start(ring(1, m, k, left))

            start(to_part(half + k, m))

        offer(k)
        return carry

    lax.fori_loop(1, half + 1, step, 0)

    def drain(k, carry):
        for copy in to_part(k, me):
            copy.wait()

        @pl.when(k < half)
        def _():
            for copy in ring(0, me, k, right):
                copy.wait_send()

        @pl.when(k < half - 1)
        def _():
            for copy in ring(1, me, k, left):
                copy.wait_send()

        return carry

    lax.fori_loop(0, chips, drain, 0)

    def arrive(k, carry):
        for j in range(2):
            points(k * 4 + j, part).wait()

            @pl.when(k < half)
            def _():
                points(k * 4 + 2 + j, part).wait()

        return carry

    points(0, part).wait()
    lax.fori_loop(1, half + 1, arrive, 0)


def edge_kernel(
    first, count, fourier, arrived, w_all, w_node, embed, mesh_features, mesh_weight, geometry, geom_weight,
    slots, receivers, noise_weight, film_weight, out,
    emb, small, left, right, msg_t, node_t, out_t, geom_b, film_b, joined, total,
):
    width = embed.shape[1]
    mesh_count = mesh_features.shape[1]
    listed = arrived.shape[0]
    chans = arrived.shape[1]
    block = right.shape[1]
    blocks = slots.shape[1] // block
    k_mesh, k_geom = mesh_weight.shape[0], geom_weight.shape[0]
    base_s = mesh_count
    base_e = mesh_count + listed

    def weight(k):
        return w_all[:, width * k : width * (k + 1)]

    left[:, base_e : base_e + width] = turned(weight(1)).astype(bf16)
    msg_t[...] = turned(weight(3)).astype(bf16)
    out_t[...] = turned(weight(4)).astype(bf16)
    node_t[...] = turned(w_node[...]).astype(bf16)
    cond = silu(jnp.sum(fourier[...] * noise_weight[...], axis=0, keepdims=True)).astype(bf16)
    cond = jnp.broadcast_to(cond.astype(f32), (8, width)).astype(bf16)
    for k in range(4):
        piece = jnp.dot(cond, film_weight[:, width * k : width * (k + 1)], preferred_element_type=f32)
        column = piece.T[:, 0:1]
        if k % 2 == 0:
            column = column + 1.0
        film_b[k] = jnp.broadcast_to(column, (width, 128))
    small[0:k_mesh] = mesh_weight[...]
    small[k_mesh : k_mesh + k_geom] = geom_weight[...]
    small[k_mesh + k_geom : 8] = jnp.zeros((8 - k_mesh - k_geom, width), f32)
    small_t = small[...].T
    pre = small_t[:, 0:1] * mesh_features[0:1, :]
    for k in range(1, k_mesh):
        pre = pre + small_t[:, k : k + 1] * mesh_features[k : k + 1, :]
    joined[0:width] = silu(pre).astype(bf16)
    recv_t = turned(weight(2)).astype(bf16)
    left[:, 0:mesh_count] = jnp.dot(recv_t, joined[0:width], preferred_element_type=f32).astype(bf16)
    for k in range(k_geom):
        geom_b[k] = jnp.broadcast_to(small_t[:, k_mesh + k : k_mesh + k + 1], (width, 128))
    rest = embed.shape[0] - first
    lead = chans - first
    emb[0:rest] = embed[first:, :].astype(f32)
    if lead > rest:
        emb[rest:lead] = jnp.zeros((lead - rest, width), f32)
    emb[lead:chans] = embed[0:first, :].astype(f32)
    emb_t = emb[...].T.astype(bf16)
    latent = silu(
        lax.dot_general(emb_t, arrived[...], (((1,), (1,)), ((), ())), preferred_element_type=f32)
    ).astype(bf16)
    send_t = turned(weight(0)).astype(bf16)
    left[:, base_s : base_s + listed] = jnp.dot(send_t, latent, preferred_element_type=f32).astype(bf16)
    total[...] = jnp.zeros_like(total)

    def add_block(b, carry):
        start = pl.multiple_of(b * block, block)
        lanes = lax.broadcasted_iota(jnp.int32, (1, block), 1) + start
        local = jnp.where(lanes < count[0], receivers[:, pl.ds(start, block)], -1)
        ids = lax.broadcasted_iota(jnp.int32, (mesh_count, block), 0)
        right[0:mesh_count] = jnp.where(ids == local, 1.0, 0.0).astype(bf16)
        ids = lax.broadcasted_iota(jnp.int32, (listed, block), 0)
        right[base_s : base_s + listed] = jnp.where(ids == slots[:, pl.ds(start, block)], 1.0, 0.0).astype(bf16)
        for j in range(block // 128):
            geo = geometry[:, pl.ds(pl.multiple_of(start + 128 * j, 128), 128)]
            pre = geom_b[0] * geo[0:1]
            for k in range(1, k_geom):
                pre = pre + geom_b[k] * geo[k : k + 1]
            right[base_e : base_e + width, 128 * j : 128 * (j + 1)] = silu(pre).astype(bf16)
        pre = jnp.dot(left[...], right[...], preferred_element_type=f32)
        hidden = silu(pre).astype(bf16)
        mixed = jnp.dot(msg_t[...], hidden, preferred_element_type=f32)
        mean = jnp.mean(mixed, axis=0, keepdims=True)
        centred = mixed - mean
        var = jnp.mean(centred * centred, axis=0, keepdims=True)
        normed = centred * lax.rsqrt(var + norm_eps)
        pieces = [
            (normed[:, 128 * j : 128 * (j + 1)] * film_b[0] + film_b[1]).astype(bf16)
            for j in range(block // 128)
        ]
        message = jnp.concatenate(pieces, axis=1)
        total[...] += lax.dot_general(
            message, right[0:mesh_count], (((1,), (1,)), ((), ())), preferred_element_type=f32
        )
        return carry

    lax.fori_loop(0, blocks, add_block, 0)
    joined[width : 2 * width] = total[...].astype(bf16)
    update = silu(jnp.dot(node_t[...], joined[...], preferred_element_type=f32)).astype(bf16)
    result = jnp.dot(out_t[...], update, preferred_element_type=f32)
    mean = jnp.mean(result, axis=0, keepdims=True)
    centred = result - mean
    var = jnp.mean(centred * centred, axis=0, keepdims=True)
    normed = centred * lax.rsqrt(var + norm_eps)
    for j in range(mesh_count // 128):
        at = slice(128 * j, 128 * (j + 1))
        piece = joined[0:width, at].astype(f32) + normed[:, at] * film_b[2] + film_b[3]
        out[at, :] = piece.T.astype(bf16)


def per_device(
    devices, conditioning, target_state, noise_sample, step_index, mesh_features, edge_geometry,
    edge_slot, edge_receiver, send_rows, edge_count, embed_weight, mesh_weight, geom_weight,
    sender_weight, edge_weight, receiver_weight, message_weight, node_weight, output_weight,
    noise_weight, film_weight,
):
    width = embed_weight.shape[1]
    freqs = noise_weight.shape[0] // 2
    frac = step_index[0].astype(f32) / (STEPS - 1)
    upper = sigma_top ** (1.0 / rho_power)
    lower = sigma_low ** (1.0 / rho_power)
    sigma = (upper + frac * (lower - upper)) ** rho_power
    angle = 0.25 * jnp.log(sigma) * (jnp.arange(freqs, dtype=f32) + 1.0)
    fourier = jnp.concatenate([jnp.sin(angle), jnp.cos(angle)])[:, None]
    scal = jnp.stack([sigma, jnp.sqrt(sigma * sigma + 1.0)])
    points = conditioning.shape[1]
    chans = (conditioning.shape[0] + target_state.shape[0] + 7) // 8 * 8
    picks = send_rows.size
    params = functools.partial(pltpu.CompilerParams, vmem_limit_bytes=LIMIT)
    outgoing = pl.pallas_call(
        pick_kernel,
        out_shape=jax.ShapeDtypeStruct((picks, chans), bf16),
        in_specs=[SMEM, VMEM, VMEM, VMEM, VMEM],
        out_specs=VMEM,
        scratch_shapes=[pltpu.VMEM((chans, points), f32)],
        compiler_params=params(),
        name="pick",
    )(scal, conditioning, target_state, noise_sample, send_rows.reshape(1, picks))
    half = devices // 4
    sem = pltpu.SemaphoreType
    arrived, w_all, w_node = pl.pallas_call(
        functools.partial(exchange_kernel, devices),
        out_shape=(
            jax.ShapeDtypeStruct((picks, chans), bf16),
            jax.ShapeDtypeStruct((devices * sender_weight.shape[0], 5 * width), bf16),
            jax.ShapeDtypeStruct((devices * node_weight.shape[0], width), bf16),
        ),
        in_specs=[VMEM] + [ANY] * 6,
        out_specs=(VMEM, VMEM, VMEM),
        scratch_shapes=[
            sem.DMA((7,)),
            sem.REGULAR((half + 1,)),
            sem.REGULAR((half + 1,)),
            sem.REGULAR,
            sem.DMA((4 * half + 4,)),
            sem.DMA((4 * half + 4,)),
            sem.DMA((2, 2, half)),
            sem.DMA((2, 2, half)),
            sem.DMA((2, 2 * half)),
            sem.DMA((2, 2 * half)),
        ],
        compiler_params=params(collective_id=0, has_side_effects=True),
        name="exchange",
    )(outgoing, sender_weight, edge_weight, receiver_weight, message_weight, output_weight, node_weight)
    slots_n = edge_slot.shape[0]
    mesh_count = mesh_features.shape[1]
    block = min(512, slots_n)
    deep = mesh_count + picks + width
    return pl.pallas_call(
        functools.partial(edge_kernel, conditioning.shape[0]),
        out_shape=jax.ShapeDtypeStruct((mesh_count, width), bf16),
        in_specs=[SMEM] + [VMEM] * 13,
        out_specs=VMEM,
        scratch_shapes=[
            pltpu.VMEM((chans, width), f32),
            pltpu.VMEM((8, width), f32),
            pltpu.VMEM((width, deep), bf16),
            pltpu.VMEM((deep, block), bf16),
            pltpu.VMEM((width, width), bf16),
            pltpu.VMEM((width, 2 * width), bf16),
            pltpu.VMEM((width, width), bf16),
            pltpu.VMEM((geom_weight.shape[0], width, 128), f32),
            pltpu.VMEM((4, width, 128), f32),
            pltpu.VMEM((2 * width, mesh_count), bf16),
            pltpu.VMEM((width, mesh_count), f32),
        ],
        compiler_params=params(),
        name="edges",
    )(
        edge_count, fourier, arrived, w_all, w_node, embed_weight, mesh_features, mesh_weight,
        edge_geometry, geom_weight, edge_slot.reshape(1, slots_n), edge_receiver.reshape(1, slots_n),
        noise_weight, film_weight,
    )


def solution(mesh):
    both = P(None, ("member", "node"))
    placed = (
        both, both, both, P("member"), P(None, "node"), P(None, "node"), P("node"), P("node"),
        P("node", None), P("node"), P(), P(), P(), P("node", None), P("node", None), P("node", None),
        P("node", None), P("node", None), P("node", None), P(), P(),
    )
    return jax.shard_map(
        functools.partial(per_device, mesh.shape["node"]),
        mesh=mesh, in_specs=placed, out_specs=P("node", "member"), check_vma=False,
    )
```

profile of v0, /device:TPU:39, one launch (start us, length us, event | category | flops | bytes accessed | tf_op | source)
XLA Modules:
  0.0 156.7 jit_solution(10683245038937658621)
XLA Ops:
  1.4 0.6 pad_maximum_fusion.scal
  2.1 0.1 maximum_bitcast_fusion
  2.2 0.7 copy.25.fourier
  2.9 0.8 copy.24
  3.7 0.7 reshape.18.rows
  4.4 2.9 %pick.1.x = bf16[1024,256]{1,0:T(8,128)(2,1)} custom-call(f32[2]{0:T(128)} %pad_maximum_fusion.scal, bf16[168,1024]{1,0:T(8,128)(2,1)} %cond.1, f32[84,1024]{1,0:T(8,128)} %target.1, f32[84,1024]{1,0:T(8,128)} %noise.1, s32[1,1024]{1,0:T(1,128)} %reshape.18.rows), custom_call_target="tpu_custom_call" | custom-call | tf_op jit(solution)/shard_map/pick/pallas_call | solution.py:335
  7.2 117.5 %exchange.1 = (bf16[1024,256]{1,0:T(8,128)(2,1)}, bf16[512,2560]{1,0:T(8,128)(2,1)}, bf16[1024,512]{1,0:T(8,128)(2,1)}) custom-call(bf16[1024,256]{1,0:T(8,128)(2,1)} %pick.1.x, bf16[8,512]{1,0:T(8,128)(2,1)} %wa.1, bf16[8,512]{1,0:T(8,128)(2,1)} %wb.1, bf16[8,512]{1,0:T(8,128)(2,1)} %wc.1, bf16[8,512]{1,0:T(8,128)(2,1)} %wd.1, bf16[8,512]{1,0:T(8,128)(2,1)} %wo.1, ...), custom_call_target="tpu_custom_call" | custom-call | tf_op jit(solution)/shard_map/exchange/pallas_call | solution.py:346
  124.8 31.9 %edges.1 = bf16[640,512]{1,0:T(8,128)(2,1)} custom-call(s32[1]{0:T(128)S(6)} %copy.27.count, f32[32,1]{1,0:T(8,128)} %copy.25.fourier, bf16[1024,256]{1,0:T(8,128)(2,1)} %get-tuple-element.8.arrived, bf16[512,2560]{1,0:T(8,128)(2,1)} %get-tuple-element.9.w_all, bf16[1024,512]{1,0:T(8,128)(2,1)} %get-tuple-element.10.w_node, bf16[252,512]{1,0:T(8,128)(2,1)} %embed.1, ...), custom_call_target="tpu_custom_call" | custom-call | tf_op jit(solution)/shard_map/edges/pallas_call | solution.py:374
  (1 shorter events, 0.0 us)
where the time goes:
time: 157 us
  Pallas kernels  152 us (97%)
  local copies, waits for them, and re-layouts  2.16 us (1%)
    pallas_call x1, Pallas kernels, per_device(): pl.pallas_call(functools.partial(exchange_kernel, devices), out_shape=(ja...  118 us
    pallas_call x1, Pallas kernels, per_device(): pl.pallas_call(functools.partial(edge_kernel, conditioning.shape[0]), out...  31.9 us

commit v1 on v0

--- a/solution.py
+++ b/solution.py
@@ -29,122 +29,136 @@
     return x.astype(f32).T
 
 
-def pick_kernel(scal, cond, target, noise, rows, out, raw):
-    chans, points = raw.shape
-    vars_ = target.shape[0]
-    lead = chans - cond.shape[0]
-    noisy = (target[...] + scal[0] * noise[...]) / scal[1]
-    raw[0:vars_] = noisy
-    if lead > vars_:
-        raw[vars_:lead] = jnp.zeros((lead - vars_, points), f32)
-    raw[lead:chans] = cond[...].astype(f32)
-    picks = rows.shape[1]
-    values = raw[...].astype(bf16)
-    ids = lax.broadcasted_iota(jnp.int32, (points, picks), 0)
-    one_hot = jnp.where(ids == rows[...], 1.0, 0.0).astype(bf16)
-    out[...] = jnp.dot(values, one_hot, preferred_element_type=f32).T.astype(bf16)
-
-
 def exchange_kernel(
-    devices, x, wa, wb, wc, wd, wo, wn, o, w_all, w_node,
-    local, ready_r, ready_l, pair, send, recv, ring_s, ring_r, part_s, part_r,
+    devices, step_index, cond, target, noise, table, wa, wb, wc, wd, wo, wn, o, w_all, w_node,
+    raw, x, local, ready_r, ready_l, pair, send, recv, long_s, long_r, near_s, near_r, side_s, side_r,
+    part_s, part_r,
 ):
     chips = devices // 2
     half = chips // 2
     me = lax.axis_index("node")
     z, c = me // 2, lax.rem(me, 2)
-    right, left = lax.rem(me + 2, devices), lax.rem(me + devices - 2, devices)
-    part = z * 2 + 1 - c
+    group = lax.axis_index("member")
+    lane = lax.rem(group, 4)
+    first = group - lane
+    sides = [first + lax.rem(lane + k, 2) + 2 * lax.rem(lane // 2 + k // 2, 2) for k in (1, 2)]
+    sides.append(first + lax.rem(lane + 1, 2) + 2 * lax.rem(lane // 2 + 1, 2))
+
+    def chip(k):
+        return lax.rem(z + k + 2 * chips, chips)
+
+    def at(k):
+        return {"node": chip(k) * 2 + c}
+
+    part = {"node": z * 2 + 1 - c}
+    right, left, far_r, far_l = at(1), at(-1), at(4), at(-4)
     barrier = pltpu.get_barrier_semaphore()
-    for t in (right, left, part):
-        pl.semaphore_signal(barrier, inc=1, device_id={"node": t}, device_id_type=MESH)
-    rows = wa.shape[0]
-    width = wa.shape[1]
+    greeted = [right, left, far_r, far_l, part] + [{"member": s} for s in sides]
+    for t in greeted:
+        pl.semaphore_signal(barrier, inc=1, device_id=t, device_id_type=MESH)
+    rows, width = wa.shape
     node_rows = wn.shape[0]
-    cap = x.shape[0] // devices
-
-    def place(n):
-        return w_all.at[pl.ds(pl.multiple_of(n * rows, rows), rows)]
-
-    def place_node(n):
-        return w_node.at[pl.ds(pl.multiple_of(n * node_rows, node_rows), node_rows)]
-
+    picks = x.shape[0]
+    cap = picks // devices
+    wide = w_all.shape[3] // 4
+    node_wide = w_node.shape[3] // 4
     own = [
-        pltpu.make_async_copy(w, place(me).at[:, width * k : width * (k + 1)], local.at[k])
+        pltpu.make_async_copy(w, w_all.at[z, c, :, width * k : width * (k + 1)], local.at[k])
         for k, w in enumerate((wa, wb, wc, wd, wo))
     ]
-    own.append(pltpu.make_async_copy(wn, place_node(me), local.at[5]))
-
-    def block(ref, n):
-        return ref.at[pl.ds(pl.multiple_of(n * cap, cap), cap)]
-
-    own.append(pltpu.make_async_copy(block(x, me), block(o, me), local.at[6]))
+    own.append(pltpu.make_async_copy(wn, w_node.at[z, c], local.at[5]))
     for copy in own:
         copy.start()
     for copy in own:
         copy.wait()
-    pl.semaphore_wait(barrier, 3)
-    pl.semaphore_signal(pair, inc=1, device_id={"node": part}, device_id_type=MESH)
-
-    def ring(direction, n, s, target):
+    refs = (
+        lambda n: w_all.at[n, c, :, pl.ds(pl.multiple_of(lane * wide, 128), wide)],
+        lambda n: w_node.at[n, c, :, pl.ds(pl.multiple_of(lane * node_wide, 128), node_wide)],
+    )
+
+    def piece(n, target, s, r):
         return [
             pltpu.make_async_remote_copy(
-                src_ref=ref(n), dst_ref=ref(n),
-                send_sem=ring_s.at[direction, k, s], recv_sem=ring_r.at[direction, k, s],
-                device_id={"node": target}, device_id_type=MESH,
+                src_ref=ref(n), dst_ref=ref(n), send_sem=s(k), recv_sem=r(k),
+                device_id=target, device_id_type=MESH,
             )
-            for k, ref in enumerate((place, place_node))
+            for k, ref in enumerate(refs)
         ]
-
-    def to_part(i, n):
-        return [
-            pltpu.make_async_remote_copy(
-                src_ref=ref(n), dst_ref=ref(n),
-                send_sem=part_s.at[k, i], recv_sem=part_r.at[k, i],
-                device_id={"node": part}, device_id_type=MESH,
-            )
-            for k, ref in enumerate((place, place_node))
-        ]
-
-    def points(i, target):
-        return pltpu.make_async_remote_copy(
-            src_ref=block(x, target), dst_ref=block(o, me),
-            send_sem=send.at[i], recv_sem=recv.at[i],
-            device_id={"node": target}, device_id_type=MESH,
-        )
 
     def start(copies):
         for copy in copies:
             copy.start()
 
-    start(ring(0, me, 0, right))
-    start(ring(1, me, 0, left))
-    pl.semaphore_wait(pair, 1)
-    points(0, part).start()
-    start(to_part(0, me))
-
-    def chip(k):
-        return lax.rem(z + k + 2 * chips, chips)
-
-    def announce(k):
-        @pl.when(k < half)
-        def _():
-            pl.semaphore_signal(ready_r.at[k + 1], inc=1, device_id={"node": left}, device_id_type=MESH)
-
-        @pl.when(k < half - 1)
-        def _():
-            pl.semaphore_signal(ready_l.at[k + 1], inc=1, device_id={"node": right}, device_id_type=MESH)
+    def landed(copies):
+        for copy in copies:
+            copy.wait_recv()
+
+    def long_hop(e, n, target):
+        return piece(n, target, lambda k: long_s.at[k, e], lambda k: long_r.at[k, e])
+
+    def near(kind, e, n):
+        target = left if kind == 2 else right
+        return piece(n, target, lambda k: near_s.at[kind, k, e], lambda k: near_r.at[kind, k, e])
+
+    def aside(n):
+        for p, s in enumerate(sides):
+            start(piece(n, {"member": s}, lambda k: side_s.at[p, k], lambda k: side_r.at[p, k]))
+
+    def spread(e, n):
+        start(near(0, e, n))
+        start(near(2, e, n))
+
+    pl.semaphore_wait(barrier, len(greeted))
+    pl.semaphore_signal(pair, inc=1, device_id=part, device_id_type=MESH)
+    start(long_hop(1, z, far_r))
+    start(long_hop(5, z, far_l))
+    spread(0, z)
+
+    vars_ = target.shape[0]
+    chans, points_n = raw.shape
+    lead = chans - cond.shape[0]
+    frac = jnp.full((1, 128), step_index[0], jnp.int32).astype(f32) / (STEPS - 1)
+    upper = sigma_top ** (1.0 / rho_power)
+    lower = sigma_low ** (1.0 / rho_power)
+    base = upper + frac * (lower - upper)
+    square = base * base
+    sigma = square * square * square * base
+    scale = jnp.sqrt(sigma * sigma + 1.0)
+    for j in range(points_n // 128):
+        lanes = slice(128 * j, 128 * (j + 1))
+        raw[0:vars_, lanes] = (target[:, lanes] + sigma * noise[:, lanes]) / scale
+    if lead > vars_:
+        raw[vars_:lead] = jnp.zeros((lead - vars_, points_n), f32)
+    raw[lead:chans] = cond[...].astype(f32)
+    spot = lax.broadcasted_iota(jnp.int32, (cap, picks), 1)
+    expand = (lax.rem(spot, cap) == lax.broadcasted_iota(jnp.int32, (cap, picks), 0)).astype(f32)
+    entries = table[...]
+    high, low = entries // 32, lax.rem(entries, 32)
+    parts = [
+        jnp.dot(part_.astype(f32).astype(bf16), expand.astype(bf16), preferred_element_type=f32)
+        for part_ in (high, low)
+    ]
+    full = parts[0] * 32.0 + parts[1]
+    spot = lax.broadcasted_iota(jnp.int32, (devices, picks), 1)
+    mine = spot // cap == lax.broadcasted_iota(jnp.int32, (devices, picks), 0)
+    wanted = jnp.sum(jnp.where(mine, full, 0.0), axis=0, keepdims=True).astype(jnp.int32)
+    values = raw[...].astype(bf16)
+    ids = lax.broadcasted_iota(jnp.int32, (points_n, picks), 0)
+    one_hot = jnp.where(ids == wanted, 1.0, 0.0).astype(bf16)
+    x[...] = jnp.dot(values, one_hot, preferred_element_type=f32).T.astype(bf16)
+
+    def block(ref, n):
+        return ref.at[pl.ds(pl.multiple_of(n * cap, cap), cap)]
+
+    o[pl.ds(pl.multiple_of(me * cap, cap), cap)] = x[pl.ds(pl.multiple_of(me * cap, cap), cap)]
+
+    def points(i, n):
+        return pltpu.make_async_remote_copy(
+            src_ref=block(x, n), dst_ref=block(o, me), send_sem=send.at[i], recv_sem=recv.at[i],
+            device_id={"node": n}, device_id_type=MESH,
+        )
 
     def offer(k):
-        @pl.when(k > 1)
-        def _():
-            pl.semaphore_wait(ready_r.at[k], 1)
-
-            @pl.when(k < half)
-            def _():
-                pl.semaphore_wait(ready_l.at[k], 1)
-
-        announce(k)
         for other in (0, 1):
             points(k * 4 + other, chip(k) * 2 + lax.rem(c + other, 2)).start()
 
@@ -152,64 +166,157 @@
             def _():
                 points(k * 4 + 2 + other, chip(-k) * 2 + lax.rem(c + other, 2)).start()
 
-    def step(k, carry):
-        n = chip(-k) * 2 + c
-        for copy in ring(0, n, k - 1, right):
-            copy.wait_recv()
-
+    def announce(k):
         @pl.when(k < half)
         def _():
-            start(ring(0, n, k, right))
-
-        start(to_part(k, n))
+            pl.semaphore_signal(ready_r.at[k + 1], inc=1, device_id=left, device_id_type=MESH)
+
+        @pl.when(k < half - 1)
+        def _():
+            pl.semaphore_signal(ready_l.at[k + 1], inc=1, device_id=right, device_id_type=MESH)
+
+    def hear(k):
+        pl.semaphore_wait(ready_r.at[k], 1)
 
         @pl.when(k < half)
         def _():
-            m = chip(k) * 2 + c
-            for copy in ring(1, m, k - 1, left):
-                copy.wait_recv()
-
-            @pl.when(k < half - 1)
+            pl.semaphore_wait(ready_l.at[k], 1)
+
+    pl.semaphore_wait(pair, 1)
+    announce(1)
+    points(0, z * 2 + 1 - c).start()
+    offer(1)
+    reach = chips // 8
+
+    def rounds(j, carry):
+        @pl.when(j <= reach)
+        def _():
+            n = chip(-4 * j)
+            landed(long_hop(j, n, far_r))
+
+            @pl.when(j < reach)
             def _():
-                start(ring(1, m, k, left))
-
-            start(to_part(half + k, m))
-
-        offer(k)
+                start(long_hop(j + 1, n, far_r))
+
+            spread(j, n)
+            aside(n)
+
+        @pl.when(j < reach)
+        def _():
+            n = chip(4 * j)
+            landed(long_hop(4 + j, n, far_l))
+
+            @pl.when(j < reach - 1)
+            def _():
+                start(long_hop(5 + j, n, far_l))
+
+            spread(4 + j, n)
+            aside(n)
+
+        def from_near(e, shift):
+            n = chip(shift - 1)
+            landed(near(0, e, n))
+            start(near(1, e, n))
+            aside(n)
+            m = chip(shift + 1)
+            landed(near(2, e, m))
+            aside(m)
+
+        def from_two(e, shift):
+            n = chip(shift - 2)
+            landed(near(1, e, n))
+            aside(n)
+
+        for t in range(4):
+            k = 4 * j - 2 + t
+
+            @pl.when(k <= half)
+            def _():
+                hear(k)
+                announce(k)
+                offer(k)
+
+        i = j - 1
+
+        @pl.when(i <= reach)
+        def _():
+            from_near(i, -4 * i)
+
+        @pl.when((i >= 1) & (i < reach))
+        def _():
+            from_near(4 + i, 4 * i)
+
+        h = j - 2
+
+        @pl.when(h >= 0)
+        def _():
+            from_two(h, -4 * h)
+
+        @pl.when((h >= 1) & (h < reach))
+        def _():
+            from_two(4 + h, 4 * h)
+
         return carry
 
-    lax.fori_loop(1, half + 1, step, 0)
-
-    def drain(k, carry):
-        for copy in to_part(k, me):
-            copy.wait()
-
-        @pl.when(k < half)
-        def _():
-            for copy in ring(0, me, k, right):
+    lax.fori_loop(1, reach + 3, rounds, 0)
+
+    def quarter(q):
+        return (
+            w_all.at[0 : chips - 1, c, :, wide * q : wide * (q + 1)],
+            w_node.at[0 : chips - 1, c, :, node_wide * q : node_wide * (q + 1)],
+        )
+
+    def side_all(p):
+        return [
+            pltpu.make_async_remote_copy(
+                src_ref=ref, dst_ref=ref, send_sem=side_s.at[p, k], recv_sem=side_r.at[p, k],
+                device_id={"member": sides[p]}, device_id_type=MESH,
+            )
+            for k, ref in enumerate(quarter(0))
+        ]
+
+    for p in range(3):
+        landed(side_all(p))
+    over = [
+        pltpu.make_async_remote_copy(
+            src_ref=ref.at[:, c], dst_ref=ref.at[:, c], send_sem=part_s.at[k], recv_sem=part_r.at[k],
+            device_id=part, device_id_type=MESH,
+        )
+        for k, ref in enumerate((w_all, w_node))
+    ]
+    start(over)
+    for p in range(3):
+        for copy in side_all(p):
+            copy.wait_send()
+
+    def sent(e, carry):
+        @pl.when(e > 0)
+        def _():
+            for copy in long_hop(e, z, far_r):
                 copy.wait_send()
 
-        @pl.when(k < half - 1)
-        def _():
-            for copy in ring(1, me, k, left):
+        for kind in range(3):
+            for copy in near(kind, e, z):
                 copy.wait_send()
 
         return carry
 
-    lax.fori_loop(0, chips, drain, 0)
+    lax.fori_loop(0, 2 * reach, sent, 0)
 
     def arrive(k, carry):
         for j in range(2):
-            points(k * 4 + j, part).wait()
+            points(k * 4 + j, me).wait()
 
             @pl.when(k < half)
             def _():
-                points(k * 4 + 2 + j, part).wait()
+                points(k * 4 + 2 + j, me).wait()
 
         return carry
 
-    points(0, part).wait()
+    points(0, me).wait()
     lax.fori_loop(1, half + 1, arrive, 0)
+    for copy in over:
+        copy.wait()
 
 
 def edge_kernel(
@@ -327,46 +434,49 @@
     sigma = (upper + frac * (lower - upper)) ** rho_power
     angle = 0.25 * jnp.log(sigma) * (jnp.arange(freqs, dtype=f32) + 1.0)
     fourier = jnp.concatenate([jnp.sin(angle), jnp.cos(angle)])[:, None]
-    scal = jnp.stack([sigma, jnp.sqrt(sigma * sigma + 1.0)])
     points = conditioning.shape[1]
     chans = (conditioning.shape[0] + target_state.shape[0] + 7) // 8 * 8
     picks = send_rows.size
     params = functools.partial(pltpu.CompilerParams, vmem_limit_bytes=LIMIT)
-    outgoing = pl.pallas_call(
-        pick_kernel,
-        out_shape=jax.ShapeDtypeStruct((picks, chans), bf16),
-        in_specs=[SMEM, VMEM, VMEM, VMEM, VMEM],
-        out_specs=VMEM,
-        scratch_shapes=[pltpu.VMEM((chans, points), f32)],
-        compiler_params=params(),
-        name="pick",
-    )(scal, conditioning, target_state, noise_sample, send_rows.reshape(1, picks))
-    half = devices // 4
+    chips = devices // 2
+    half = chips // 2
     sem = pltpu.SemaphoreType
+    rows, node_rows = sender_weight.shape[0], node_weight.shape[0]
     arrived, w_all, w_node = pl.pallas_call(
         functools.partial(exchange_kernel, devices),
         out_shape=(
             jax.ShapeDtypeStruct((picks, chans), bf16),
-            jax.ShapeDtypeStruct((devices * sender_weight.shape[0], 5 * width), bf16),
-            jax.ShapeDtypeStruct((devices * node_weight.shape[0], width), bf16),
+            jax.ShapeDtypeStruct((chips, 2, rows, 5 * width), bf16),
+            jax.ShapeDtypeStruct((chips, 2, node_rows, width), bf16),
         ),
-        in_specs=[VMEM] + [ANY] * 6,
+        in_specs=[SMEM] + [VMEM] * 4 + [ANY] * 6,
         out_specs=(VMEM, VMEM, VMEM),
         scratch_shapes=[
-            sem.DMA((7,)),
+            pltpu.VMEM((chans, points), f32),
+            pltpu.VMEM((picks, chans), bf16),
+            sem.DMA((6,)),
             sem.REGULAR((half + 1,)),
             sem.REGULAR((half + 1,)),
             sem.REGULAR,
             sem.DMA((4 * half + 4,)),
             sem.DMA((4 * half + 4,)),
-            sem.DMA((2, 2, half)),
-            sem.DMA((2, 2, half)),
-            sem.DMA((2, 2 * half)),
-            sem.DMA((2, 2 * half)),
+            sem.DMA((2, chips // 4)),
+            sem.DMA((2, chips // 4)),
+            sem.DMA((3, 2, chips // 4)),
+            sem.DMA((3, 2, chips // 4)),
+            sem.DMA((3, 2)),
+            sem.DMA((3, 2)),
+            sem.DMA((2,)),
+            sem.DMA((2,)),
         ],
         compiler_params=params(collective_id=0, has_side_effects=True),
         name="exchange",
-    )(outgoing, sender_weight, edge_weight, receiver_weight, message_weight, output_weight, node_weight)
+    )(
+        step_index, conditioning, target_state, noise_sample, send_rows,
+        sender_weight, edge_weight, receiver_weight, message_weight, output_weight, node_weight,
+    )
+    w_all = w_all.reshape(devices * rows, 5 * width)
+    w_node = w_node.reshape(devices * node_rows, width)
     slots_n = edge_slot.shape[0]
     mesh_count = mesh_features.shape[1]
     block = min(512, slots_n)

time: 157 us -> 131 us (0.83)
  Pallas kernels: 152 us -> 127 us
    pallas_call x1, Pallas kernels: 118 us -> 95.1 us  [per_device(): pl.pallas_call(functools.partial(exchange_kernel, devices), out_shape=(ja...]
    pallas_call x1 -> x0, Pallas kernels: 2.89 us -> none  [per_device(): pl.pallas_call(pick_kernel, out_shape=jax.ShapeDtypeStruct((picks, chans)...]
where the time goes in v1:
time: 131 us
  Pallas kernels  127 us (97%)
  local copies, waits for them, and re-layouts  2.1 us (2%)
  between operations  1.35 us (1%)
    pallas_call x1, Pallas kernels, per_device(): pl.pallas_call(functools.partial(exchange_kernel, devices), out_shape=(ja...  95.1 us
    pallas_call x1, Pallas kernels, per_device(): pl.pallas_call(functools.partial(edge_kernel, conditioning.shape[0]), out...  31.9 us

profile of v1, /device:TPU:39, one launch (start us, length us, event | category | flops | bytes accessed | tf_op | source)
XLA Modules:
  0.0 130.6 jit_solution(10082948037775599628)
XLA Ops:
  1.4 0.1 maximum_bitcast_fusion
  1.5 0.7 copy.23.fourier
  2.2 1.4 %copy.22.table = s32[64,16]{1,0:T(8,128)} copy(s32[64,16]{0,1:T(8,128)} %param.29) | data formatting | bytes 8192 | tf_op args[8]
  3.6 95.1 %exchange.1 = (bf16[1024,256]{1,0:T(8,128)(2,1)}, bf16[32,2,8,2560]{3,2,1,0:T(8,128)(2,1)}, bf16[32,2,16,512]{3,2,1,0:T(8,128)(2,1)}) custom-call(s32[1]{0:T(128)S(6)} %copy.24.step_index, bf16[168,1024]{1,0:T(8,128)(2,1)} %cond.1, f32[84,1024]{1,0:T(8,128)} %target.1, f32[84,1024]{1,0:T(8,128)} %noise.1, s32[64,16]{1,0:T(8,128)} %copy.22.table, ...), custom_call_target="tpu_custom_call" | custom-call | tf_op jit(solution)/shard_map/exchange/pallas_call | solution.py:445
  98.7 31.9 %edges.1 = bf16[640,512]{1,0:T(8,128)(2,1)} custom-call(s32[1]{0:T(128)S(6)} %copy.25.count, f32[32,1]{1,0:T(8,128)} %copy.23.fourier, bf16[1024,256]{1,0:T(8,128)(2,1)} %get-tuple-element.8.arrived, bf16[512,2560]{1,0:T(8,128)(2,1)} %bitcast.7, bf16[1024,512]{1,0:T(8,128)(2,1)} %bitcast.8, bf16[252,512]{1,0:T(8,128)(2,1)} %embed.1, f32[3,640]{1,0:T(4,128)} %mesh_features.1, ...), custom_call_target="tpu_custom_call" | custom-call | tf_op jit(solution)/shard_map/edges/pallas_call | solution.py:484
  (1 shorter events, 0.0 us)

commit v2 on v1

v2 whole, which is shorter than its diff:
```python
import functools

import jax
import jax.numpy as jnp
from jax import lax
from jax.experimental import pallas as pl
from jax.experimental.pallas import tpu as pltpu
from jax.sharding import PartitionSpec as P

STEPS = 20
sigma_top = 80.0
sigma_low = 0.03
rho_power = 7.0
norm_eps = 1e-05
MESH = pl.DeviceIdType.MESH
VMEM = pl.BlockSpec(memory_space=pltpu.VMEM)
SMEM = pl.BlockSpec(memory_space=pltpu.SMEM)
ANY = pl.BlockSpec(memory_space=pl.ANY)
LIMIT = 60 * 1024 * 1024
f32, bf16 = jnp.float32, jnp.bfloat16


def silu(x):
    half = 0.5 * x
    return half + half * jnp.tanh(half)


def turned(x):
    return x.astype(f32).T


def encoder_kernel(
    devices, step_index, count, cond, target, noise, table, embed, mesh_features, mesh_weight, geometry,
    geom_weight, slots, receivers, noise_weight, film_weight, wa, wb, wc, wd, wo, wn, out,
    raw, x, o, w_all, w_node, emb, small, embedded, pick_s, pick_r, partial, sender_t, recv_t,
    edge_t, msg_t, node_t, out_t, geom_b, film_b, joined, total,
    local, ready_r, ready_l, pair, send, recv, long_s, long_r, near_s, near_r, side_s, side_r,
    part_s, part_r,
):
    chips = devices // 2
    half = chips // 2
    me = lax.axis_index("node")
    z, c = me // 2, lax.rem(me, 2)
    group = lax.axis_index("member")
    lane = lax.rem(group, 4)
    first = group - lane
    sides = [first + lax.rem(lane + k, 2) + 2 * lax.rem(lane // 2 + k // 2, 2) for k in (1, 2)]
    sides.append(first + lax.rem(lane + 1, 2) + 2 * lax.rem(lane // 2 + 1, 2))

    def chip(k):
        return lax.rem(z + k + 2 * chips, chips)

    def at(k):
        return {"node": chip(k) * 2 + c}

    part = {"node": z * 2 + 1 - c}
    right, left, far_r, far_l = at(1), at(-1), at(4), at(-4)
    barrier = pltpu.get_barrier_semaphore()
    greeted = [right, left, far_r, far_l, part] + [{"member": s} for s in sides]
    for t in greeted:
        pl.semaphore_signal(barrier, inc=1, device_id=t, device_id_type=MESH)
    rows, width = wa.shape
    node_rows = wn.shape[0]
    picks = x.shape[0]
    cap = picks // devices
    wide = w_all.shape[3] // 4
    node_wide = w_node.shape[3] // 4
    own = [
        pltpu.make_async_copy(w, w_all.at[z, c, :, width * k : width * (k + 1)], local.at[k])
        for k, w in enumerate((wa, wb, wc, wd, wo))
    ]
    own.append(pltpu.make_async_copy(wn, w_node.at[z, c], local.at[5]))
    for copy in own:
        copy.start()
    for copy in own:
        copy.wait()
    refs = (
        lambda n: w_all.at[n, c, :, pl.ds(pl.multiple_of(lane * wide, 128), wide)],
        lambda n: w_node.at[n, c, :, pl.ds(pl.multiple_of(lane * node_wide, 128), node_wide)],
    )

    def piece(n, target, s, r):
        return [
            pltpu.make_async_remote_copy(
                src_ref=ref(n), dst_ref=ref(n), send_sem=s(k), recv_sem=r(k),
                device_id=target, device_id_type=MESH,
            )
            for k, ref in enumerate(refs)
        ]

    def start(copies):
        for copy in copies:
            copy.start()

    def landed(copies):
        for copy in copies:
            copy.wait_recv()

    def long_hop(e, n, target):
        return piece(n, target, lambda k: long_s.at[k, e], lambda k: long_r.at[k, e])

    def near(kind, e, n):
        target = left if kind == 2 else right
        return piece(n, target, lambda k: near_s.at[kind, k, e], lambda k: near_r.at[kind, k, e])

    def aside(n):
        for p, s in enumerate(sides):
            start(piece(n, {"member": s}, lambda k: side_s.at[p, k], lambda k: side_r.at[p, k]))

    def spread(e, n):
        start(near(0, e, n))
        start(near(2, e, n))

    pl.semaphore_wait(barrier, len(greeted))
    pl.semaphore_signal(pair, inc=1, device_id=part, device_id_type=MESH)
    start(long_hop(1, z, far_r))
    start(long_hop(5, z, far_l))
    spread(0, z)

    def announce(k):
        @pl.when(k < half)
        def _():
            pl.semaphore_signal(ready_r.at[k + 1], inc=1, device_id=left, device_id_type=MESH)

        @pl.when(k < half - 1)
        def _():
            pl.semaphore_signal(ready_l.at[k + 1], inc=1, device_id=right, device_id_type=MESH)

    pl.semaphore_wait(pair, 1)
    announce(1)

    vars_ = target.shape[0]
    chans, points_n = raw.shape
    lead = chans - cond.shape[0]
    frac = jnp.full((1, 128), step_index[0], jnp.int32).astype(f32) / (STEPS - 1)
    upper = sigma_top ** (1.0 / rho_power)
    lower = sigma_low ** (1.0 / rho_power)
    base = upper + frac * (lower - upper)
    square = base * base
    sigma = square * square * square * base
    scale = jnp.sqrt(sigma * sigma + 1.0)
    for j in range(points_n // 128):
        lanes = slice(128 * j, 128 * (j + 1))
        raw[0:vars_, lanes] = (target[:, lanes] + sigma * noise[:, lanes]) / scale
    if lead > vars_:
        raw[vars_:lead] = jnp.zeros((lead - vars_, points_n), f32)
    raw[lead:chans] = cond[...].astype(f32)
    spot = lax.broadcasted_iota(jnp.int32, (devices, picks), 1)
    expand = jnp.where(spot // cap == lax.broadcasted_iota(jnp.int32, (devices, picks), 0), 1.0, 0.0).astype(bf16)
    entries = table[...]
    high, low = [
        jnp.dot(half_.astype(f32).astype(bf16), expand, preferred_element_type=f32)
        for half_ in (entries // 32, lax.rem(entries, 32))
    ]
    spot = lax.broadcasted_iota(jnp.int32, (cap, picks), 1)
    mine = lax.rem(spot, cap) == lax.broadcasted_iota(jnp.int32, (cap, picks), 0)
    wanted = jnp.sum(jnp.where(mine, high * 32.0 + low, 0.0), axis=0, keepdims=True).astype(jnp.int32)
    values = raw[...].astype(bf16)
    ids = lax.broadcasted_iota(jnp.int32, (points_n, picks), 0)
    one_hot = jnp.where(ids == wanted, 1.0, 0.0).astype(bf16)
    x[...] = jnp.dot(values, one_hot, preferred_element_type=f32).T.astype(bf16)

    def block(ref, n):
        return ref.at[pl.ds(pl.multiple_of(n * cap, cap), cap)]

    o[pl.ds(pl.multiple_of(me * cap, cap), cap)] = x[pl.ds(pl.multiple_of(me * cap, cap), cap)]

    def points(i, n):
        return pltpu.make_async_remote_copy(
            src_ref=block(x, n), dst_ref=block(o, me), send_sem=send.at[i], recv_sem=recv.at[i],
            device_id={"node": n}, device_id_type=MESH,
        )

    def offer(k):
        for other in (0, 1):
            points(k * 4 + other, chip(k) * 2 + lax.rem(c + other, 2)).start()

            @pl.when(k < half)
            def _():
                points(k * 4 + 2 + other, chip(-k) * 2 + lax.rem(c + other, 2)).start()

    def hear(k):
        pl.semaphore_wait(ready_r.at[k], 1)

        @pl.when(k < half)
        def _():
            pl.semaphore_wait(ready_l.at[k], 1)

    points(0, z * 2 + 1 - c).start()
    offer(1)
    reach = chips // 8

    def rounds(j, carry):
        @pl.when(j <= reach)
        def _():
            n = chip(-4 * j)
            landed(long_hop(j, n, far_r))

            @pl.when(j < reach)
            def _():
                start(long_hop(j + 1, n, far_r))

            spread(j, n)
            aside(n)

        @pl.when(j < reach)
        def _():
            n = chip(4 * j)
            landed(long_hop(4 + j, n, far_l))

            @pl.when(j < reach - 1)
            def _():
                start(long_hop(5 + j, n, far_l))

            spread(4 + j, n)
            aside(n)

        def from_near(e, shift):
            n = chip(shift - 1)
            landed(near(0, e, n))
            start(near(1, e, n))
            aside(n)
            m = chip(shift + 1)
            landed(near(2, e, m))
            aside(m)

        def from_two(e, shift):
            n = chip(shift - 2)
            landed(near(1, e, n))
            aside(n)

        for t in range(4):
            k = 4 * j - 2 + t

            @pl.when(k <= half)
            def _():
                hear(k)
                announce(k)
                offer(k)

        i = j - 1

        @pl.when(i <= reach)
        def _():
            from_near(i, -4 * i)

        @pl.when((i >= 1) & (i < reach))
        def _():
            from_near(4 + i, 4 * i)

        h = j - 2

        @pl.when(h >= 0)
        def _():
            from_two(h, -4 * h)

        @pl.when((h >= 1) & (h < reach))
        def _():
            from_two(4 + h, 4 * h)

        return carry

    lax.fori_loop(1, reach + 3, rounds, 0)

    width = embed.shape[1]
    mesh_count = mesh_features.shape[1]
    batch = min(512, slots.shape[1])
    blocks = slots.shape[1] // batch
    k_mesh, k_geom = mesh_weight.shape[0], geom_weight.shape[0]
    small[0:k_mesh] = mesh_weight[...]
    small[k_mesh : k_mesh + k_geom] = geom_weight[...]
    small[k_mesh + k_geom : 8] = jnp.zeros((8 - k_mesh - k_geom, width), f32)
    small_t = small[...].T
    for k in range(k_geom):
        geom_b[k] = jnp.broadcast_to(small_t[:, k_mesh + k : k_mesh + k + 1], (width, 128))

    def prepare(b, carry):
        first_ = pl.multiple_of(b * batch, batch)
        lanes = lax.broadcasted_iota(jnp.int32, (1, batch), 1) + first_
        here = jnp.where(lanes < count[0], receivers[:, pl.ds(first_, batch)], -1)
        ids = lax.broadcasted_iota(jnp.int32, (mesh_count, batch), 0)
        pick_r[:, pl.ds(first_, batch)] = jnp.where(ids == here, 1.0, 0.0).astype(bf16)
        ids = lax.broadcasted_iota(jnp.int32, (picks, batch), 0)
        pick_s[:, pl.ds(first_, batch)] = jnp.where(ids == slots[:, pl.ds(first_, batch)], 1.0, 0.0).astype(bf16)
        for j in range(batch // 128):
            spot_ = pl.ds(pl.multiple_of(first_ + 128 * j, 128), 128)
            geo = geometry[:, spot_]
            pre = geom_b[0] * geo[0:1]
            for k in range(1, k_geom):
                pre = pre + geom_b[k] * geo[k : k + 1]
            embedded[:, spot_] = silu(pre).astype(bf16)
        return carry

    lax.fori_loop(0, blocks, prepare, 0)

    def quarter(q):
        return (
            w_all.at[0 : chips - 1, c, :, wide * q : wide * (q + 1)],
            w_node.at[0 : chips - 1, c, :, node_wide * q : node_wide * (q + 1)],
        )

    def side_all(p):
        return [
            pltpu.make_async_remote_copy(
                src_ref=ref, dst_ref=ref, send_sem=side_s.at[p, k], recv_sem=side_r.at[p, k],
                device_id={"member": sides[p]}, device_id_type=MESH,
            )
            for k, ref in enumerate(quarter(0))
        ]

    for p in range(3):
        landed(side_all(p))
    over = [
        pltpu.make_async_remote_copy(
            src_ref=ref.at[:, c], dst_ref=ref.at[:, c], send_sem=part_s.at[k], recv_sem=part_r.at[k],
            device_id=part, device_id_type=MESH,
        )
        for k, ref in enumerate((w_all, w_node))
    ]
    start(over)
    angle = 0.25 * jnp.log(sigma[:, 0:1]) * (
        lax.broadcasted_iota(jnp.int32, (noise_weight.shape[0] // 2, 1), 0).astype(f32) + 1.0
    )
    freqs = noise_weight.shape[0] // 2
    level = jnp.sum(jnp.sin(angle) * noise_weight[0:freqs], axis=0, keepdims=True)
    level = level + jnp.sum(jnp.cos(angle) * noise_weight[freqs:], axis=0, keepdims=True)
    level = silu(level).astype(bf16).astype(f32)
    level = jnp.broadcast_to(level, (8, width)).astype(bf16)
    for k in range(4):
        film = jnp.dot(level, film_weight[:, width * k : width * (k + 1)], preferred_element_type=f32)
        column = film.T[:, 0:1]
        if k % 2 == 0:
            column = column + 1.0
        film_b[k] = jnp.broadcast_to(column, (width, 128))
    pre = small_t[:, 0:1] * mesh_features[0:1, :]
    for k in range(1, k_mesh):
        pre = pre + small_t[:, k : k + 1] * mesh_features[k : k + 1, :]
    joined[0:width] = silu(pre).astype(bf16)
    cond_rows = cond.shape[0]
    rest = embed.shape[0] - cond_rows
    emb[0:rest] = embed[cond_rows:, :].astype(f32)
    if lead > rest:
        emb[rest:lead] = jnp.zeros((lead - rest, width), f32)
    emb[lead:chans] = embed[0:cond_rows, :].astype(f32)
    emb_t = emb[...].T.astype(bf16)
    total[...] = jnp.zeros_like(total)
    landed(over)

    def weight(k):
        return w_all[:, :, :, width * k : width * (k + 1)].reshape(width, width)

    edge_t[...] = turned(weight(1)).astype(bf16)
    recv_t[...] = jnp.dot(
        turned(weight(2)).astype(bf16), joined[0:width], preferred_element_type=f32
    ).astype(bf16)

    def before_senders(b, carry):
        spot_ = pl.ds(pl.multiple_of(b * batch, batch), batch)
        value = jnp.dot(edge_t[...], embedded[:, spot_], preferred_element_type=f32)
        partial[:, spot_] = value + jnp.dot(recv_t[...], pick_r[:, spot_], preferred_element_type=f32)
        return carry

    lax.fori_loop(0, blocks, before_senders, 0)
    send_t = turned(weight(0)).astype(bf16)
    msg_t[...] = turned(weight(3)).astype(bf16)
    out_t[...] = turned(weight(4)).astype(bf16)
    node_t[...] = turned(w_node[...].reshape(2 * width, width)).astype(bf16)

    def arrive(k, carry):
        for j in range(2):
            points(k * 4 + j, me).wait_recv()

            @pl.when(k < half)
            def _():
                points(k * 4 + 2 + j, me).wait_recv()

        return carry

    points(0, me).wait_recv()
    lax.fori_loop(1, half + 1, arrive, 0)
    latent = silu(
        lax.dot_general(emb_t, o[...], (((1,), (1,)), ((), ())), preferred_element_type=f32)
    ).astype(bf16)
    sender_t[...] = jnp.dot(send_t, latent, preferred_element_type=f32).astype(bf16)

    def norm(values):
        mean = jnp.mean(values, axis=0, keepdims=True)
        centred = values - mean
        var = jnp.mean(centred * centred, axis=0, keepdims=True)
        return centred * lax.rsqrt(var + norm_eps)

    def add_block(b, carry):
        spot_ = pl.ds(pl.multiple_of(b * batch, batch), batch)
        pre = partial[:, spot_] + jnp.dot(sender_t[...], pick_s[:, spot_], preferred_element_type=f32)
        hidden = silu(pre).astype(bf16)
        normed = norm(jnp.dot(msg_t[...], hidden, preferred_element_type=f32))
        message = jnp.concatenate(
            [
                (normed[:, 128 * j : 128 * (j + 1)] * film_b[0] + film_b[1]).astype(bf16)
                for j in range(batch // 128)
            ],
            axis=1,
        )
        total[...] += lax.dot_general(
            message, pick_r[:, spot_], (((1,), (1,)), ((), ())), preferred_element_type=f32
        )
        return carry

    lax.fori_loop(0, blocks, add_block, 0)
    for p in range(3):
        for copy in side_all(p):
            copy.wait_send()

    def sent(e, carry):
        @pl.when(e > 0)
        def _():
            for copy in long_hop(e, z, far_r):
                copy.wait_send()

        for kind in range(3):
            for copy in near(kind, e, z):
                copy.wait_send()

        return carry

    lax.fori_loop(0, 2 * reach, sent, 0)

    for copy in over:
        copy.wait_send()


    def left_(k, carry):
        for j in range(2):
            points(k * 4 + j, me).wait_send()

            @pl.when(k < half)
            def _():
                points(k * 4 + 2 + j, me).wait_send()

        return carry

    points(0, me).wait_send()
    lax.fori_loop(1, half + 1, left_, 0)
    joined[width : 2 * width] = total[...].astype(bf16)
    update = silu(jnp.dot(node_t[...], joined[...], preferred_element_type=f32)).astype(bf16)
    normed = norm(jnp.dot(out_t[...], update, preferred_element_type=f32))
    for j in range(mesh_count // 128):
        lanes = slice(128 * j, 128 * (j + 1))
        value = joined[0:width, lanes].astype(f32) + normed[:, lanes] * film_b[2] + film_b[3]
        out[lanes, :] = value.T.astype(bf16)


def per_device(
    devices, conditioning, target_state, noise_sample, step_index, mesh_features, edge_geometry,
    edge_slot, edge_receiver, send_rows, edge_count, embed_weight, mesh_weight, geom_weight,
    sender_weight, edge_weight, receiver_weight, message_weight, node_weight, output_weight,
    noise_weight, film_weight,
):
    width = embed_weight.shape[1]
    points = conditioning.shape[1]
    chans = (conditioning.shape[0] + target_state.shape[0] + 7) // 8 * 8
    picks = send_rows.size
    slots_n = edge_slot.shape[0]
    mesh_count = mesh_features.shape[1]
    chips = devices // 2
    half = chips // 2
    sem = pltpu.SemaphoreType
    rows, node_rows = sender_weight.shape[0], node_weight.shape[0]
    return pl.pallas_call(
        functools.partial(encoder_kernel, devices),
        out_shape=jax.ShapeDtypeStruct((mesh_count, width), bf16),
        in_specs=[SMEM] * 2 + [VMEM] * 13 + [ANY] * 6,
        out_specs=VMEM,
        scratch_shapes=[
            pltpu.VMEM((chans, points), f32),
            pltpu.VMEM((picks, chans), bf16),
            pltpu.VMEM((picks, chans), bf16),
            pltpu.VMEM((chips, 2, rows, 5 * width), bf16),
            pltpu.VMEM((chips, 2, node_rows, width), bf16),
            pltpu.VMEM((chans, width), f32),
            pltpu.VMEM((8, width), f32),
            pltpu.VMEM((width, slots_n), bf16),
            pltpu.VMEM((picks, slots_n), bf16),
            pltpu.VMEM((mesh_count, slots_n), bf16),
            pltpu.VMEM((width, slots_n), f32),
            pltpu.VMEM((width, picks), bf16),
            pltpu.VMEM((width, mesh_count), bf16),
            pltpu.VMEM((width, width), bf16),
            pltpu.VMEM((width, width), bf16),
            pltpu.VMEM((width, 2 * width), bf16),
            pltpu.VMEM((width, width), bf16),
            pltpu.VMEM((geom_weight.shape[0], width, 128), f32),
            pltpu.VMEM((4, width, 128), f32),
            pltpu.VMEM((2 * width, mesh_count), bf16),
            pltpu.VMEM((width, mesh_count), f32),
            sem.DMA((6,)),
            sem.REGULAR((half + 1,)),
            sem.REGULAR((half + 1,)),
            sem.REGULAR,
            sem.DMA((4 * half + 4,)),
            sem.DMA((4 * half + 4,)),
            sem.DMA((2, chips // 4)),
            sem.DMA((2, chips // 4)),
            sem.DMA((3, 2, chips // 4)),
            sem.DMA((3, 2, chips // 4)),
            sem.DMA((3, 2)),
            sem.DMA((3, 2)),
            sem.DMA((2,)),
            sem.DMA((2,)),
        ],
        compiler_params=pltpu.CompilerParams(
            vmem_limit_bytes=LIMIT, collective_id=0, has_side_effects=True
        ),
        name="encoder",
    )(
        step_index, edge_count, conditioning, target_state, noise_sample, send_rows.T, embed_weight,
        mesh_features, mesh_weight, edge_geometry, geom_weight, edge_slot.reshape(1, slots_n),
        edge_receiver.reshape(1, slots_n), noise_weight, film_weight, sender_weight, edge_weight,
        receiver_weight, message_weight, output_weight, node_weight,
    )


def solution(mesh):
    both = P(None, ("member", "node"))
    placed = (
        both, both, both, P("member"), P(None, "node"), P(None, "node"), P("node"), P("node"),
        P("node", None), P("node"), P(), P(), P(), P("node", None), P("node", None), P("node", None),
        P("node", None), P("node", None), P("node", None), P(), P(),
    )
    return jax.shard_map(
        functools.partial(per_device, mesh.shape["node"]),
        mesh=mesh, in_specs=placed, out_specs=P("node", "member"), check_vma=False,
    )
```

time: 131 us -> 128 us (0.977)
  Pallas kernels: 127 us -> 124 us
    pallas_call x2 -> x1, Pallas kernels: 127 us -> 124 us  [per_device(): pl.pallas_call(functools.partial(encoder_kernel, devices), out_shape=jax....]
where the time goes in v2:
time: 128 us; the launch traced here: 127 us
  Pallas kernels  124 us (97%)
  local copies, waits for them, and re-layouts  1.97 us (2%)
  between operations  1.3 us (1%)
    pallas_call x1, Pallas kernels, per_device(): pl.pallas_call(functools.partial(encoder_kernel, devices), out_shape=jax....  124 us

profile of v2, /device:TPU:39, one launch (start us, length us, event | category | flops | bytes accessed | tf_op | source)
XLA Modules:
  0.0 127.4 jit_solution(3898011237108897288)
XLA Ops:
  1.3 124.1 %encoder.1 = bf16[640,512]{1,0:T(8,128)(2,1)} custom-call(s32[1]{0:T(128)S(6)} %copy.23.step_index, s32[1]{0:T(128)S(6)} %copy.24.count, bf16[168,1024]{1,0:T(8,128)(2,1)} %cond.1, f32[84,1024]{1,0:T(8,128)} %target.1, f32[84,1024]{1,0:T(8,128)} %noise.1, s32[16,64]{1,0:T(8,128)} %bitcast.5, bf16[252,512]{1,0:T(8,128)(2,1)} %embed.1, ...), custom_call_target="tpu_custom_call" | custom-call | tf_op jit(solution)/shard_map/encoder/pallas_call | solution.py:469
  125.4 2.0 %copy.25 = bf16[640,512]{1,0:T(8,128)(2,1)} copy(bf16[640,512]{1,0:T(8,128)(2,1)} %encoder.1) | data formatting | bytes 1310720

commit v3 on v2

--- a/solution.py
+++ b/solution.py
@@ -30,11 +30,11 @@
 
 
 def encoder_kernel(
-    devices, step_index, count, cond, target, noise, table, embed, mesh_features, mesh_weight, geometry,
-    geom_weight, slots, receivers, noise_weight, film_weight, wa, wb, wc, wd, wo, wn, out,
-    raw, x, o, w_all, w_node, emb, small, embedded, pick_s, pick_r, partial, sender_t, recv_t,
+    devices, step_index, count, table, mesh_features, mesh_weight, geom_weight, slots, receivers,
+    noise_weight, cond_in, target_in, noise_in, geometry_in, embed_in, film_in, wa, wb, wc, wd, wo, wn, out,
+    cond, target, noise, geometry, embed, film_weight, raw, x, o, w_all, w_node, emb, small, embedded, pick_s, pick_r, partial, sender_t, recv_t,
     edge_t, msg_t, node_t, out_t, geom_b, film_b, joined, total,
-    local, ready_r, ready_l, pair, send, recv, long_s, long_r, near_s, near_r, side_s, side_r,
+    local, fetch, ready_r, ready_l, pair, pair_done, send, recv, long_s, long_r, near_s, near_r, side_s, side_r,
     part_s, part_r,
 ):
     chips = devices // 2
@@ -59,6 +59,15 @@
     greeted = [right, left, far_r, far_l, part] + [{"member": s} for s in sides]
     for t in greeted:
         pl.semaphore_signal(barrier, inc=1, device_id=t, device_id_type=MESH)
+    fetched = [
+        pltpu.make_async_copy(src, dst, fetch.at[k])
+        for k, (src, dst) in enumerate(
+            (
+                (target_in, target), (noise_in, noise), (cond_in, cond),
+                (geometry_in, geometry), (embed_in, embed), (film_in, film_weight),
+            )
+        )
+    ]
     rows, width = wa.shape
     node_rows = wn.shape[0]
     picks = x.shape[0]
@@ -70,7 +79,7 @@
         for k, w in enumerate((wa, wb, wc, wd, wo))
     ]
     own.append(pltpu.make_async_copy(wn, w_node.at[z, c], local.at[5]))
-    for copy in own:
+    for copy in own + fetched:
         copy.start()
     for copy in own:
         copy.wait()
@@ -129,6 +138,8 @@
     pl.semaphore_wait(pair, 1)
     announce(1)
 
+    for copy in fetched[:3]:
+        copy.wait()
     vars_ = target.shape[0]
     chans, points_n = raw.shape
     lead = chans - cond.shape[0]
@@ -236,7 +247,6 @@
             def _():
                 hear(k)
                 announce(k)
-                offer(k)
 
         i = j - 1
 
@@ -258,15 +268,31 @@
         def _():
             from_two(4 + h, 4 * h)
 
+        @pl.when(j <= reach)
+        def _():
+            offer(2 * j)
+            offer(2 * j + 1)
+
         return carry
 
     lax.fori_loop(1, reach + 3, rounds, 0)
+
+    pl.semaphore_signal(pair_done, inc=1, device_id=part, device_id_type=MESH)
+    pl.semaphore_wait(pair_done, 1)
+
+    def rest(t, carry):
+        offer(half - t)
+        return carry
+
+    lax.fori_loop(0, half - 2 * reach - 1, rest, 0)
 
     width = embed.shape[1]
     mesh_count = mesh_features.shape[1]
     batch = min(512, slots.shape[1])
     blocks = slots.shape[1] // batch
     k_mesh, k_geom = mesh_weight.shape[0], geom_weight.shape[0]
+    for copy in fetched[3:]:
+        copy.wait()
     small[0:k_mesh] = mesh_weight[...]
     small[k_mesh : k_mesh + k_geom] = geom_weight[...]
     small[k_mesh + k_geom : 8] = jnp.zeros((8 - k_mesh - k_geom, width), f32)
@@ -291,7 +317,7 @@
             embedded[:, spot_] = silu(pre).astype(bf16)
         return carry
 
-    lax.fori_loop(0, blocks, prepare, 0)
+    lax.fori_loop(0, blocks // 2, prepare, 0)
 
     def quarter(q):
         return (
@@ -318,6 +344,7 @@
         for k, ref in enumerate((w_all, w_node))
     ]
     start(over)
+    lax.fori_loop(blocks // 2, blocks, prepare, 0)
     angle = 0.25 * jnp.log(sigma[:, 0:1]) * (
         lax.broadcasted_iota(jnp.int32, (noise_weight.shape[0] // 2, 1), 0).astype(f32) + 1.0
     )
@@ -469,9 +496,15 @@
     return pl.pallas_call(
         functools.partial(encoder_kernel, devices),
         out_shape=jax.ShapeDtypeStruct((mesh_count, width), bf16),
-        in_specs=[SMEM] * 2 + [VMEM] * 13 + [ANY] * 6,
+        in_specs=[SMEM] * 2 + [VMEM] * 7 + [ANY] * 12,
         out_specs=VMEM,
         scratch_shapes=[
+            pltpu.VMEM(conditioning.shape, bf16),
+            pltpu.VMEM(target_state.shape, f32),
+            pltpu.VMEM(noise_sample.shape, f32),
+            pltpu.VMEM(edge_geometry.shape, f32),
+            pltpu.VMEM(embed_weight.shape, bf16),
+            pltpu.VMEM(film_weight.shape, bf16),
             pltpu.VMEM((chans, points), f32),
             pltpu.VMEM((picks, chans), bf16),
             pltpu.VMEM((picks, chans), bf16),
@@ -494,8 +527,10 @@
             pltpu.VMEM((2 * width, mesh_count), bf16),
             pltpu.VMEM((width, mesh_count), f32),
             sem.DMA((6,)),
+            sem.DMA((6,)),
             sem.REGULAR((half + 1,)),
             sem.REGULAR((half + 1,)),
+            sem.REGULAR,
             sem.REGULAR,
             sem.DMA((4 * half + 4,)),
             sem.DMA((4 * half + 4,)),
@@ -513,10 +548,10 @@
         ),
         name="encoder",
     )(
-        step_index, edge_count, conditioning, target_state, noise_sample, send_rows.T, embed_weight,
-        mesh_features, mesh_weight, edge_geometry, geom_weight, edge_slot.reshape(1, slots_n),
-        edge_receiver.reshape(1, slots_n), noise_weight, film_weight, sender_weight, edge_weight,
-        receiver_weight, message_weight, output_weight, node_weight,
+        step_index, edge_count, send_rows.T, mesh_features, mesh_weight, geom_weight,
+        edge_slot.reshape(1, slots_n), edge_receiver.reshape(1, slots_n), noise_weight,
+        conditioning, target_state, noise_sample, edge_geometry, embed_weight, film_weight,
+        sender_weight, edge_weight, receiver_weight, message_weight, output_weight, node_weight,
     )
 
 

time: 128 us -> 119 us (0.930)
  Pallas kernels: 124 us -> 115 us
    pallas_call x1, Pallas kernels: 124 us -> 115 us  [per_device(): pl.pallas_call(functools.partial(encoder_kernel, devices), out_shape=jax....]
where the time goes in v3:
time: 119 us
  Pallas kernels  115 us (97%)
  local copies, waits for them, and re-layouts  1.97 us (2%)
  between operations  1.3 us (1%)
    pallas_call x1, Pallas kernels, per_device(): pl.pallas_call(functools.partial(encoder_kernel, devices), out_shape=jax....  115 us

profile of v3, /device:TPU:39, one launch (start us, length us, event | category | flops | bytes accessed | tf_op | source)
XLA Modules:
  0.0 118.8 jit_solution(16462351789456350759)
XLA Ops:
  1.3 115.5 %encoder.1 = bf16[640,512]{1,0:T(8,128)(2,1)} custom-call(s32[1]{0:T(128)S(6)} %copy.23.step_index, s32[1]{0:T(128)S(6)} %copy.24.count, s32[16,64]{1,0:T(8,128)} %bitcast.5, f32[3,640]{1,0:T(4,128)} %mesh_features.1, f32[3,512]{1,0:T(4,128)} %mesh_weight.1, f32[4,512]{1,0:T(4,128)} %geom_weight.1, s32[1,4096]{1,0:T(1,128)} %bitcast.3, s32[1,4096]{1,0:T(1,128)} %bitcast.4, ...), custom_call_target="tpu_custom_call" | custom-call | tf_op jit(solution)/shard_map/encoder/pallas_call | solution.py:496
  116.8 2.0 %copy.25 = bf16[640,512]{1,0:T(8,128)(2,1)} copy(bf16[640,512]{1,0:T(8,128)(2,1)} %encoder.1) | data formatting | bytes 1310720

commit v4 on v3

--- a/solution.py
+++ b/solution.py
@@ -33,7 +33,7 @@
     devices, step_index, count, table, mesh_features, mesh_weight, geom_weight, slots, receivers,
     noise_weight, cond_in, target_in, noise_in, geometry_in, embed_in, film_in, wa, wb, wc, wd, wo, wn, out,
     cond, target, noise, geometry, embed, film_weight, raw, x, o, w_all, w_node, emb, small, embedded, pick_s, pick_r, partial, sender_t, recv_t,
-    edge_t, msg_t, node_t, out_t, geom_b, film_b, joined, total,
+    edge_t, msg_t, node_t, out_t, geom_b, film_b, joined, total, emb_t, send_t,
     local, fetch, ready_r, ready_l, pair, pair_done, send, recv, long_s, long_r, near_s, near_r, side_s, side_r,
     part_s, part_r,
 ):
@@ -174,21 +174,26 @@
     def block(ref, n):
         return ref.at[pl.ds(pl.multiple_of(n * cap, cap), cap)]
 
-    o[pl.ds(pl.multiple_of(me * cap, cap), cap)] = x[pl.ds(pl.multiple_of(me * cap, cap), cap)]
-
-    def points(i, n):
+    around = chips // 4
+    o[pl.ds(pl.multiple_of((around * 2 + c) * cap, cap), cap)] = x[pl.ds(pl.multiple_of(me * cap, cap), cap)]
+
+    def points(i, n, seen=0):
         return pltpu.make_async_remote_copy(
-            src_ref=block(x, n), dst_ref=block(o, me), send_sem=send.at[i], recv_sem=recv.at[i],
+            src_ref=block(x, n), dst_ref=block(o, seen * 2 + c), send_sem=send.at[i], recv_sem=recv.at[i],
             device_id={"node": n}, device_id_type=MESH,
         )
 
     def offer(k):
         for other in (0, 1):
-            points(k * 4 + other, chip(k) * 2 + lax.rem(c + other, 2)).start()
+            points(
+                k * 4 + other, chip(k) * 2 + lax.rem(c + other, 2), lax.rem(around - k + chips, chips)
+            ).start()
 
             @pl.when(k < half)
             def _():
-                points(k * 4 + 2 + other, chip(-k) * 2 + lax.rem(c + other, 2)).start()
+                points(
+                    k * 4 + 2 + other, chip(-k) * 2 + lax.rem(c + other, 2), lax.rem(around + k, chips)
+                ).start()
 
     def hear(k):
         pl.semaphore_wait(ready_r.at[k], 1)
@@ -197,7 +202,7 @@
         def _():
             pl.semaphore_wait(ready_l.at[k], 1)
 
-    points(0, z * 2 + 1 - c).start()
+    points(0, z * 2 + 1 - c, around).start()
     offer(1)
     reach = chips // 8
 
@@ -306,8 +311,9 @@
         here = jnp.where(lanes < count[0], receivers[:, pl.ds(first_, batch)], -1)
         ids = lax.broadcasted_iota(jnp.int32, (mesh_count, batch), 0)
         pick_r[:, pl.ds(first_, batch)] = jnp.where(ids == here, 1.0, 0.0).astype(bf16)
+        shifted = lax.rem(slots[:, pl.ds(first_, batch)] + (chips + around - z) * 2 * cap, picks)
         ids = lax.broadcasted_iota(jnp.int32, (picks, batch), 0)
-        pick_s[:, pl.ds(first_, batch)] = jnp.where(ids == slots[:, pl.ds(first_, batch)], 1.0, 0.0).astype(bf16)
+        pick_s[:, pl.ds(first_, batch)] = jnp.where(ids == shifted, 1.0, 0.0).astype(bf16)
         for j in range(batch // 128):
             spot_ = pl.ds(pl.multiple_of(first_ + 128 * j, 128), 128)
             geo = geometry[:, spot_]
@@ -369,7 +375,7 @@
     if lead > rest:
         emb[rest:lead] = jnp.zeros((lead - rest, width), f32)
     emb[lead:chans] = embed[0:cond_rows, :].astype(f32)
-    emb_t = emb[...].T.astype(bf16)
+    emb_t[...] = emb[...].T.astype(bf16)
     total[...] = jnp.zeros_like(total)
     landed(over)
 
@@ -381,21 +387,49 @@
         turned(weight(2)).astype(bf16), joined[0:width], preferred_element_type=f32
     ).astype(bf16)
 
+    near_rows = picks // 2
+
+    def embed_rows(rows_):
+        latent = silu(
+            lax.dot_general(emb_t[...], o[rows_], (((1,), (1,)), ((), ())), preferred_element_type=f32)
+        ).astype(bf16)
+        sender_t[:, rows_] = jnp.dot(send_t[...], latent, preferred_element_type=f32).astype(bf16)
+
+    send_t[...] = turned(weight(0)).astype(bf16)
+
+    def arrive_near(k, carry):
+        for j in range(2):
+            points(k * 4 + j, me).wait_recv()
+
+            @pl.when(k < around)
+            def _():
+                points(k * 4 + 2 + j, me).wait_recv()
+
+        return carry
+
+    points(0, me).wait_recv()
+    lax.fori_loop(1, around + 1, arrive_near, 0)
+    embed_rows(slice(0, near_rows))
+
     def before_senders(b, carry):
         spot_ = pl.ds(pl.multiple_of(b * batch, batch), batch)
         value = jnp.dot(edge_t[...], embedded[:, spot_], preferred_element_type=f32)
-        partial[:, spot_] = value + jnp.dot(recv_t[...], pick_r[:, spot_], preferred_element_type=f32)
+        value = value + jnp.dot(recv_t[...], pick_r[:, spot_], preferred_element_type=f32)
+        partial[:, spot_] = value + jnp.dot(
+            sender_t[:, 0:near_rows], pick_s[0:near_rows, spot_], preferred_element_type=f32
+        )
         return carry
 
     lax.fori_loop(0, blocks, before_senders, 0)
-    send_t = turned(weight(0)).astype(bf16)
     msg_t[...] = turned(weight(3)).astype(bf16)
     out_t[...] = turned(weight(4)).astype(bf16)
     node_t[...] = turned(w_node[...].reshape(2 * width, width)).astype(bf16)
 
-    def arrive(k, carry):
+    def arrive_far(k, carry):
         for j in range(2):
-            points(k * 4 + j, me).wait_recv()
+            @pl.when(k > around)
+            def _():
+                points(k * 4 + j, me).wait_recv()
 
             @pl.when(k < half)
             def _():
@@ -403,12 +437,8 @@
 
         return carry
 
-    points(0, me).wait_recv()
-    lax.fori_loop(1, half + 1, arrive, 0)
-    latent = silu(
-        lax.dot_general(emb_t, o[...], (((1,), (1,)), ((), ())), preferred_element_type=f32)
-    ).astype(bf16)
-    sender_t[...] = jnp.dot(send_t, latent, preferred_element_type=f32).astype(bf16)
+    lax.fori_loop(around, half + 1, arrive_far, 0)
+    embed_rows(slice(near_rows, picks))
 
     def norm(values):
         mean = jnp.mean(values, axis=0, keepdims=True)
@@ -418,7 +448,9 @@
 
     def add_block(b, carry):
         spot_ = pl.ds(pl.multiple_of(b * batch, batch), batch)
-        pre = partial[:, spot_] + jnp.dot(sender_t[...], pick_s[:, spot_], preferred_element_type=f32)
+        pre = partial[:, spot_] + jnp.dot(
+            sender_t[:, near_rows:], pick_s[near_rows:, spot_], preferred_element_type=f32
+        )
         hidden = silu(pre).astype(bf16)
         normed = norm(jnp.dot(msg_t[...], hidden, preferred_element_type=f32))
         message = jnp.concatenate(
@@ -526,6 +558,8 @@
             pltpu.VMEM((4, width, 128), f32),
             pltpu.VMEM((2 * width, mesh_count), bf16),
             pltpu.VMEM((width, mesh_count), f32),
+            pltpu.VMEM((width, chans), bf16),
+            pltpu.VMEM((width, width), bf16),
             sem.DMA((6,)),
             sem.DMA((6,)),
             sem.REGULAR((half + 1,)),

time: 119 us -> 117 us (0.983)
  Pallas kernels: 115 us -> 113 us
    pallas_call x1, Pallas kernels: 115 us -> 113 us  [per_device(): pl.pallas_call(functools.partial(encoder_kernel, devices), out_shape=jax....]
where the time goes in v4:
time: 117 us; the launch traced here: 116 us
  Pallas kernels  113 us (97%)
  local copies, waits for them, and re-layouts  1.97 us (2%)
  between operations  1.3 us (1%)
    pallas_call x1, Pallas kernels, per_device(): pl.pallas_call(functools.partial(encoder_kernel, devices), out_shape=jax....  113 us

profile of v4, /device:TPU:39, one launch (start us, length us, event | category | flops | bytes accessed | tf_op | source)
XLA Modules:
  0.0 116.1 jit_solution(2171502716471140611)
XLA Ops:
  1.3 112.8 %encoder.1 = bf16[640,512]{1,0:T(8,128)(2,1)} custom-call(s32[1]{0:T(128)S(6)} %copy.23.step_index, s32[1]{0:T(128)S(6)} %copy.24.count, s32[16,64]{1,0:T(8,128)} %bitcast.5, f32[3,640]{1,0:T(4,128)} %mesh_features.1, f32[3,512]{1,0:T(4,128)} %mesh_weight.1, f32[4,512]{1,0:T(4,128)} %geom_weight.1, s32[1,4096]{1,0:T(1,128)} %bitcast.3, s32[1,4096]{1,0:T(1,128)} %bitcast.4, ...), custom_call_target="tpu_custom_call" | custom-call | tf_op jit(solution)/shard_map/encoder/pallas_call | solution.py:528
  114.1 2.0 %copy.25 = bf16[640,512]{1,0:T(8,128)(2,1)} copy(bf16[640,512]{1,0:T(8,128)(2,1)} %encoder.1) | data formatting | bytes 1310720
